TPU v7x, 32 devices: a whole 2x2x4 slice. The times are simulated.
32 devices in a mesh: lat: 4 (over x, core), lon: 8 (over z, y).
Axes of the slice: x: 2, y: 2, z: 4, core: 2. Of those that a mesh axis runs over, the one named last changes fastest.
Arguments:
- background: bfloat16 [16, 256, 2560], P('lat', 'lon'), may hold values from -6 to 6
- band_cols: int32 [16], P('lat'), may hold values from 20 to 256, as said below
- obs_col: int32 [16, 512], P('lat', 'lon'), may hold values from 0 to 255, as said below
- obs_lev: int32 [16, 512], P('lat', 'lon'), may hold values from 0 to 39
- obs_mask: int32 [16, 512], P('lat', 'lon'), may hold values from 0 to 1, as said below
- innov: float32 [16, 512], P('lat', 'lon'), may hold values from -9 to 9
- obs_var: float32 [16, 512], P('lat', 'lon'), may hold values from 0.25 to 2.5
Outputs:
- analysis: bfloat16 [16, 256, 2560], P('lat', 'lon')
Inputs may be any that keep to these rules, and one draw needn't show every extreme that they name: Band 0 has 20 columns, band 16 // 2 has 160 columns and the last band 256; columns from band_cols on are padding. `obs_col`: slot i of a band lies in the columns from i // 64 * 32 to that plus 32 - 1. An observation in use lies below its band's band_cols. No column holds more than 4 observations in use, and some column of every band holds exactly 4. `obs_mask`: 1 marks an observation in use.
All inputs are finite; a program needn't handle non-finite values.
Results may differ from a plain program's by a relative error of at most 0.0061.
Values may be sent and summed in bfloat16 or wider, within the bound.
A program may use at most 128 MiB of HBM per device.

v0:
```python
import functools

import jax
import jax.numpy as jnp
from jax import lax
from jax.experimental import pallas as pl
from jax.experimental.pallas import tpu as pltpu
from jax.sharding import PartitionSpec as P

K = 64
LEV = 40
RADIUS = 8
ITERS = 4
GROUP = 4
LANES = 128
F32 = jnp.float32
BF16 = jnp.bfloat16
MESH = pl.DeviceIdType.MESH


def taper_weights(radius):
    half_width = radius / 2.0
    tapering = []
    for offset in range(radius):
        distance = offset / half_width
        if distance <= 1.0:
            weight = (
                ((-0.25 * distance + 0.5) * distance + 0.625) * distance**3
                - 5.0 / 3.0 * distance**2
                + 1.0
            )
        else:
            weight = (
                (((distance / 12.0 - 0.5) * distance + 0.625) * distance + 5.0 / 3.0) * distance**2
                - 5.0 * distance
                + 4.0
                - 2.0 / (3.0 * distance)
            )
        tapering.append(weight)
    return tapering


def dot(left, right):
    return jnp.dot(left, right, preferred_element_type=F32)


def iota(shape, dim):
    return lax.broadcasted_iota(jnp.int32, shape, dim)


def exchange_kernel(
    lats,
    lons,
    x_ref,
    col_ref,
    lev_ref,
    mask_ref,
    innov_ref,
    var_ref,
    pay_ref,
    shift_ref,
    stat_buf,
    pay_send,
    pay_recv,
    stat_send,
    stat_recv,
):
    total = lats * lons
    lat, lon = lax.axis_index("lat"), lax.axis_index("lon")
    me = lat * lons + lon
    barrier = pltpu.get_barrier_semaphore()

    def greet(step, carry):
        other = lax.rem(me + step, total)
        pl.semaphore_signal(
            barrier,
            inc=1,
            device_id=(other // lons, lax.rem(other, lons)),
            device_id_type=MESH,
        )
        return carry

    lax.fori_loop(1, total, greet, 0)

    bands, columns, width = x_ref.shape
    obs = col_ref.shape[1]
    half = obs // 2
    pairs = width // LANES
    local = (col_ref[...] - lon * columns).astype(F32)
    mask = mask_ref[...].astype(F32)
    scale = jnp.sqrt(mask / var_ref[...])
    params = jnp.concatenate([local, lev_ref[...].astype(F32), scale, innov_ref[...]], axis=0)
    params = jnp.concatenate([params, jnp.zeros((LANES - 4 * bands, obs), F32)], axis=0)
    params = jnp.concatenate([params, jnp.zeros((LANES, LANES - obs), F32)], axis=1)
    upright = jnp.transpose(params)[:obs]
    lane = iota((half, LANES), 1)
    col_ids = iota((obs, columns), 1)
    tags = jnp.zeros((half, LANES), F32)
    centre_sum = jnp.zeros((obs, 1), F32)
    spread_sum = jnp.zeros((obs, K), F32)
    for b in range(bands):
        col = upright[:, b : b + 1]
        lev = upright[:, bands + b : bands + b + 1].astype(jnp.int32)
        onehot = jnp.where(col_ids == col.astype(jnp.int32), 1.0, 0.0).astype(BF16)
        pair = lax.shift_right_logical(lev, 1)
        found = jnp.zeros((obs, LANES), F32)
        for p in range(pairs):
            got = dot(onehot, x_ref[b, :, p * LANES : (p + 1) * LANES])
            found = jnp.where(pair == p, got, found)
        picked = jnp.where((lev & 1) == 1, found[:, K:], found[:, :K])
        anomaly = picked - jnp.mean(picked, axis=1, keepdims=True)
        depart = upright[:, 2 * bands + b : 2 * bands + b + 1] * (
            anomaly - upright[:, 3 * bands + b : 3 * bands + b + 1]
        )
        depart = depart.astype(BF16).astype(F32)
        centre = jnp.mean(depart, axis=1, keepdims=True)
        spread = depart - centre
        centre_sum = centre_sum + centre * centre
        spread_sum = spread_sum + spread * spread
        packed = jnp.concatenate([depart[:half], depart[half:]], axis=1)
        pay_ref[lon, b * half : (b + 1) * half, :] = packed.astype(BF16)
        tags = jnp.where(lane == 2 * b, col[:half], tags)
        tags = jnp.where(lane == 2 * b + 1, col[half:], tags)
    pay_ref[lon, bands * half :, :] = tags.astype(BF16)
    numerator = jnp.sum(centre_sum, axis=0, keepdims=True)
    spread_row = jnp.sum(spread_sum, axis=0, keepdims=True)
    mask_row = jnp.sum(mask, axis=0, keepdims=True)
    denominator = jnp.sum(spread_row / (K - 1), axis=1, keepdims=True) + jnp.sum(
        mask_row, axis=1, keepdims=True
    )
    stat_lane = iota((8, LANES), 1)
    stat_buf[me] = jnp.where(stat_lane == 0, numerator, denominator)

    pl.semaphore_wait(barrier, total - 1)

    def stat_copy(slot, step, other):
        return pltpu.make_async_remote_copy(
            src_ref=stat_buf.at[slot],
            dst_ref=stat_buf.at[slot],
            send_sem=stat_send.at[step],
            recv_sem=stat_recv.at[slot],
            device_id=(other // lons, lax.rem(other, lons)),
            device_id_type=MESH,
        )

    def pay_copy(slot, step, other):
        return pltpu.make_async_remote_copy(
            src_ref=pay_ref.at[slot],
            dst_ref=pay_ref.at[slot],
            send_sem=pay_send.at[step],
            recv_sem=pay_recv.at[slot],
            device_id=(lat, other),
            device_id_type=MESH,
        )

    def send_stat(step, carry):
        stat_copy(me, step, lax.rem(me + step, total)).start()
        return carry

    def send_pay(step, carry):
        pay_copy(lon, step, lax.rem(lon + step, lons)).start()
        return carry

    lax.fori_loop(1, lons, send_pay, 0)
    lax.fori_loop(1, total, send_stat, 0)

    def take_stat(step, carry):
        stat_copy(me, step, lax.rem(me + step, total)).wait_send()
        source = lax.rem(me + total - step, total)
        stat_copy(source, step, source).wait_recv()
        return carry

    def take_pay(step, carry):
        pay_copy(lon, step, lax.rem(lon + step, lons)).wait_send()
        source = lax.rem(lon + lons - step, lons)
        pay_copy(source, step, source).wait_recv()
        return carry

    lax.fori_loop(1, total, take_stat, 0)
    lax.fori_loop(1, lons, take_pay, 0)
    stats = jnp.sum(stat_buf[...], axis=0)
    inflation = (stats[:, 0:1] + 1e-06) / stats[:, 1:2]
    shift_ref[...] = jnp.broadcast_to((K - 1) / inflation, (8, LANES))


def analysis_kernel(x_ref, pay_ref, shift_ref, cols_ref, out_ref, tags_s, xs, ys, w_s, st_s, rhs_s, gs):
    lon = lax.axis_index("lon")
    bands, columns, width = x_ref.shape
    lons, pay_rows, _ = pay_ref.shape
    half = pay_rows // (bands + 1)
    held = lons * half
    obs = 2 * held
    pairs = width // LANES
    groups = columns // GROUP
    span = GROUP * K
    tapering = taper_weights(RADIUS)
    tags = jnp.concatenate(
        [pay_ref[j, bands * half :, :] for j in range(lons)], axis=0
    ).astype(F32)
    tags_s[...] = jnp.transpose(tags)
    shift = shift_ref[0:1, 0:1]
    low = iota((K, LANES), 1) < K
    low_f = jnp.where(low, 1.0, 0.0)
    low_b = low_f.astype(BF16)
    high_b = (1.0 - low_f).astype(BF16)
    zero_b = jnp.zeros((K, LANES), BF16)
    eye = jnp.where(iota((K, span), 0) == iota((K, span), 1) % K, 1.0, 0.0)

    def block_diag(mat):
        left, right = mat[:, :LANES], mat[:, LANES:]
        return jnp.concatenate(
            [
                jnp.concatenate([left * low_b, zero_b], axis=1),
                jnp.concatenate([left * high_b, zero_b], axis=1),
                jnp.concatenate([zero_b, right * low_b], axis=1),
                jnp.concatenate([zero_b, right * high_b], axis=1),
            ],
            axis=0,
        )

    ones_bd = block_diag(jnp.ones((K, span), BF16))

    def one_band(b, carry):
        count = cols_ref[b]
        for p in range(pairs):
            xs[:, p, :] = x_ref[b, :, p * LANES : (p + 1) * LANES].astype(F32)
        start = pl.multiple_of(b * half, half)
        block = jnp.concatenate(
            [pay_ref[j, pl.ds(start, half), :] for j in range(lons)], axis=0
        ).astype(F32)
        turned = jnp.transpose(block)
        depart_t = jnp.concatenate([turned[:K], turned[K:]], axis=1)
        centre = jnp.mean(depart_t, axis=0, keepdims=True)
        st_s[...] = depart_t - centre
        rolled = pltpu.roll(block, K, 1)
        low_h = iota((held, LANES), 1) < K
        rhs = jnp.concatenate(
            [jnp.where(low_h, block, rolled), jnp.where(low_h, rolled, block)], axis=0
        )
        rhs_s[...] = (rhs - jnp.mean(rhs, axis=1, keepdims=True)).astype(BF16)
        col = jnp.concatenate(
            [tags_s[pl.ds(2 * b, 1), :], tags_s[pl.ds(2 * b + 1, 1), :]], axis=1
        )
        owner = (iota((1, obs), 1) % held) // half
        source = col.astype(jnp.int32) + owner * columns
        away = source - (lon * columns + iota((columns, obs), 0))
        away = jnp.where(2 * away > count, away - count, away)
        away = jnp.where(2 * away < -count, away + count, away)
        away = jnp.abs(away)
        weight = jnp.zeros((columns, obs), F32)
        for t in range(RADIUS):
            weight = jnp.where(away == t, tapering[t], weight)
        w_s[...] = weight
        mean_rows = dot((weight * -centre).astype(BF16), rhs_s[...])
        squares = []
        for g in range(groups):
            parts = []
            for c in range(g * GROUP, (g + 1) * GROUP):
                weighted = (st_s[...] * w_s[c : c + 1, :]).astype(BF16)
                parts.append(dot(weighted, rhs_s[...]))
            cat = jnp.concatenate(
                [jnp.where(low, parts[0], parts[1]), jnp.where(low, parts[2], parts[3])], axis=1
            )
            gs[g] = cat
            system = cat + shift * eye
            squares.append(jnp.sum(system * system, axis=0, keepdims=True))
        squares = jnp.concatenate(squares, axis=0)
        coarse = squares.astype(BF16)
        fine = (squares - coarse.astype(F32)).astype(BF16)
        sums = dot(jnp.concatenate([coarse, fine], axis=0), ones_bd)
        frob = jnp.sqrt(sums[:groups] + sums[groups:])
        inv_frob = 1.0 / frob
        scaling = jnp.sqrt((K - 1.0) * inv_frob)
        beta_all = 1.0 - shift * inv_frob
        batch = min(4, groups)
        for first in range(0, groups, batch):
            ids = range(first, first + batch)
            beta = [beta_all[g : g + 1] for g in ids]
            dev = [gs[g] * -inv_frob[g : g + 1] for g in ids]
            zeta = [1.0 + 0.5 * be for be in beta]
            root = [0.5 * d for d in dev]
            for it in range(ITERS):
                narrow = [d.astype(BF16) for d in dev]
                fixed = [block_diag(n) for n in narrow]
                if it == 0:
                    square = [dot(n, f) for n, f in zip(narrow, fixed)]
                elif it + 1 < ITERS:
                    both = [
                        dot(jnp.concatenate([n, r.astype(BF16)], axis=0), f)
                        for n, r, f in zip(narrow, root, fixed)
                    ]
                    square = [x[:K] for x in both]
                    prod = [x[K:] for x in both]
                else:
                    prod = [dot(r.astype(BF16), f) for r, f in zip(root, fixed)]
                if it > 0:
                    root = [
                        (1.0 + 0.5 * be) * r + (0.5 * ze) * d + 0.5 * x
                        for be, r, ze, d, x in zip(beta, root, zeta, dev, prod)
                    ]
                    zeta = [ze * (1.0 + 0.5 * be) for ze, be in zip(zeta, beta)]
                if it + 1 < ITERS:
                    square = [2.0 * be * d + s for be, d, s in zip(beta, dev, square)]
                    cube = [dot(s.astype(BF16), f) for s, f in zip(square, fixed)]
                    dev = [
                        (0.75 + 0.25 * be) * s + (0.25 * be * be) * d + 0.25 * c
                        for be, s, d, c in zip(beta, square, dev, cube)
                    ]
                    beta = [be * be * (0.75 + 0.25 * be) for be in beta]
            for i, g in enumerate(ids):
                c0 = g * GROUP
                row = jnp.concatenate(
                    [
                        jnp.where(low[:1], mean_rows[c0 : c0 + 1], mean_rows[c0 + 1 : c0 + 2]),
                        jnp.where(low[:1], mean_rows[c0 + 2 : c0 + 3], mean_rows[c0 + 3 : c0 + 4]),
                    ],
                    axis=1,
                )
                full = zeta[i] * eye + root[i]
                rows = jnp.broadcast_to(row, (8, span)).astype(BF16)
                half_step = zeta[i] * row + dot(rows, block_diag(root[i].astype(BF16)))[:1]
                shifted = dot((full * half_step).astype(BF16), ones_bd)
                scale = scaling[g : g + 1]
                mix = (
                    scale * full
                    + (1.0 - scale * zeta[i]) * (1.0 / K)
                    + shifted * inv_frob[g : g + 1]
                )
                for pair in range(GROUP // 2):
                    two = mix[:, pair * LANES : (pair + 1) * LANES]
                    swapped = pltpu.roll(two, K, 1).astype(BF16)
                    two = two.astype(BF16)
                    for side in range(2):
                        c = c0 + 2 * pair + side
                        upper, lower = (two, swapped) if side == 0 else (swapped, two)
                        apply = jnp.concatenate([upper * low_b, lower * high_b], axis=0)
                        ys[c] = dot(xs[c].astype(BF16), apply)
        keep = lon * columns + iota((columns, LANES), 0) < count
        for p in range(pairs):
            out_ref[b, :, p * LANES : (p + 1) * LANES] = jnp.where(
                keep, ys[:, p, :], 0.0
            ).astype(BF16)
        return carry

    lax.fori_loop(0, bands, one_band, 0)


def per_device(lats, lons, background, band_cols, obs_col, obs_lev, obs_mask, innov, obs_var):
    bands, columns, width = background.shape
    obs = obs_col.shape[1]
    half = obs // 2
    pay_rows = (bands + 1) * half
    total = lats * lons
    vmem = pl.BlockSpec(memory_space=pltpu.VMEM)
    pay, shift = pl.pallas_call(
        functools.partial(exchange_kernel, lats, lons),
        out_shape=(
            jax.ShapeDtypeStruct((lons, pay_rows, LANES), BF16),
            jax.ShapeDtypeStruct((8, LANES), F32),
        ),
        in_specs=[vmem] * 6,
        out_specs=(vmem, vmem),
        scratch_shapes=[
            pltpu.VMEM((total, 8, LANES), F32),
            pltpu.SemaphoreType.DMA((lons,)),
            pltpu.SemaphoreType.DMA((lons,)),
            pltpu.SemaphoreType.DMA((total,)),
            pltpu.SemaphoreType.DMA((total,)),
        ],
        compiler_params=pltpu.CompilerParams(collective_id=0, has_side_effects=True),
        name="exchange",
    )(background, obs_col, obs_lev, obs_mask, innov, obs_var)
    held = lons * half
    pairs = width // LANES
    return pl.pallas_call(
        analysis_kernel,
        out_shape=jax.ShapeDtypeStruct(background.shape, BF16),
        in_specs=[vmem, vmem, vmem, pl.BlockSpec(memory_space=pltpu.SMEM)],
        out_specs=vmem,
        scratch_shapes=[
            pltpu.VMEM((LANES, held), F32),
            pltpu.VMEM((columns, pairs, LANES), F32),
            pltpu.VMEM((columns, pairs, LANES), F32),
            pltpu.VMEM((columns, 2 * held), F32),
            pltpu.VMEM((K, 2 * held), F32),
            pltpu.VMEM((2 * held, LANES), BF16),
            pltpu.VMEM((columns // GROUP, K, GROUP * K), F32),
        ],
        name="analysis",
    )(background, pay, shift, band_cols)


def solution(mesh):
    placed = (P("lat", "lon", None), P("lat")) + (P("lat", "lon"),) * 5
    return jax.shard_map(
        functools.partial(per_device, mesh.shape["lat"], mesh.shape["lon"]),
        mesh=mesh,
        in_specs=placed,
        out_specs=P("lat", "lon", None),
        check_vma=False,
    )
```

profile of v0, /device:TPU:0, one launch (start us, length us, event | category | flops | bytes accessed | tf_op | source)
XLA Modules:
  0.0 49.6 jit_solution(5635611293203980268)
XLA Ops:
  0.0 21.8 %exchange.1 = (bf16[8,160,128]{2,1,0:T(8,128)(2,1)}, f32[8,128]{1,0:T(8,128)}) custom-call(bf16[4,32,2560]{2,1,0:T(8,128)(2,1)} %x_ref.3, s32[4,64]{1,0:T(4,128)} %col_ref.1, s32[4,64]{1,0:T(4,128)} %lev_ref.1, s32[4,64]{1,0:T(4,128)} %mask_ref.1, f32[4,64]{1,0:T(4,128)} %innov_ref.1, f32[4,64]{1,0:T(4,128)} %var_ref.1), custom_call_target="tpu_custom_call" | custom-call | tf_op jit(solution)/shard_map/exchange/pallas_call | solution.py:355
  21.8 27.8 %analysis.1 = bf16[4,32,2560]{2,1,0:T(8,128)(2,1)} custom-call(bf16[4,32,2560]{2,1,0:T(8,128)(2,1)} %x_ref.3, bf16[8,160,128]{2,1,0:T(8,128)(2,1)} %get-tuple-element.7.pay_ref, f32[8,128]{1,0:T(8,128)} %get-tuple-element.8.shift_ref, s32[4]{0:T(128)} %cols_ref.1), custom_call_target="tpu_custom_call" | custom-call | tf_op jit(solution)/shard_map/analysis/pallas_call | solution.py:375
where the time goes:
time: 49.8 us; the launch traced here: 49.6 us
  Pallas kernels  49.6 us (100%)
    pallas_call x1, Pallas kernels, per_device(): pl.pallas_call(analysis_kernel, out_shape=jax.ShapeDtypeStruct(background...  27.8 us
    pallas_call x1, Pallas kernels, per_device(): pl.pallas_call(functools.partial(exchange_kernel, lats, lons), out_shape=...  21.8 us

commit v1 on v0

--- a/solution.py
+++ b/solution.py
@@ -12,6 +12,9 @@
 RADIUS = 8
 ITERS = 4
 GROUP = 4
+OC = 4
+END_SLOTS = 32
+FAR = 1 << 20
 LANES = 128
 F32 = jnp.float32
 BF16 = jnp.bfloat16
@@ -57,45 +60,64 @@
     mask_ref,
     innov_ref,
     var_ref,
-    pay_ref,
+    cols_ref,
+    own_ref,
+    side_ref,
     shift_ref,
-    stat_buf,
-    pay_send,
-    pay_recv,
-    stat_send,
-    stat_recv,
+    ends_buf,
+    near_buf,
+    tail_buf,
+    lat_buf,
+    lon_buf,
+    near_send,
+    near_recv,
+    head_send,
+    head_recv,
+    tail_send,
+    tail_recv,
+    lat_send,
+    lat_recv,
+    lon_send,
+    lon_recv,
 ):
-    total = lats * lons
     lat, lon = lax.axis_index("lat"), lax.axis_index("lon")
-    me = lat * lons + lon
     barrier = pltpu.get_barrier_semaphore()
-
-    def greet(step, carry):
-        other = lax.rem(me + step, total)
+    near_buf[...] = jnp.zeros_like(near_buf)
+    tail_buf[...] = jnp.zeros_like(tail_buf)
+
+    def greet_lon(step, carry):
         pl.semaphore_signal(
-            barrier,
-            inc=1,
-            device_id=(other // lons, lax.rem(other, lons)),
-            device_id_type=MESH,
+            barrier, inc=1, device_id=(lat, lax.rem(lon + step, lons)), device_id_type=MESH
         )
         return carry
 
-    lax.fori_loop(1, total, greet, 0)
+    def greet_lat(step, carry):
+        pl.semaphore_signal(
+            barrier, inc=1, device_id=(lax.rem(lat + step, lats), lon), device_id_type=MESH
+        )
+        return carry
+
+    lax.fori_loop(1, lons, greet_lon, 0)
+    lax.fori_loop(1, lats, greet_lat, 0)
 
     bands, columns, width = x_ref.shape
     obs = col_ref.shape[1]
     half = obs // 2
     pairs = width // LANES
-    local = (col_ref[...] - lon * columns).astype(F32)
+    reach = RADIUS - 1
+    ends = END_SLOTS
+    first = lon * columns
+    local_int = col_ref[...] - first
+    local = local_int.astype(F32)
     mask = mask_ref[...].astype(F32)
     scale = jnp.sqrt(mask / var_ref[...])
     params = jnp.concatenate([local, lev_ref[...].astype(F32), scale, innov_ref[...]], axis=0)
     params = jnp.concatenate([params, jnp.zeros((LANES - 4 * bands, obs), F32)], axis=0)
     params = jnp.concatenate([params, jnp.zeros((LANES, LANES - obs), F32)], axis=1)
     upright = jnp.transpose(params)[:obs]
-    lane = iota((half, LANES), 1)
     col_ids = iota((obs, columns), 1)
-    tags = jnp.zeros((half, LANES), F32)
+    earlier = iota((obs, obs), 0) < iota((obs, obs), 1)
+    slot_ids = iota((ends, obs), 0)
     centre_sum = jnp.zeros((obs, 1), F32)
     spread_sum = jnp.zeros((obs, K), F32)
     for b in range(bands):
@@ -109,19 +131,33 @@
             found = jnp.where(pair == p, got, found)
         picked = jnp.where((lev & 1) == 1, found[:, K:], found[:, :K])
         anomaly = picked - jnp.mean(picked, axis=1, keepdims=True)
-        depart = upright[:, 2 * bands + b : 2 * bands + b + 1] * (
-            anomaly - upright[:, 3 * bands + b : 3 * bands + b + 1]
-        )
-        depart = depart.astype(BF16).astype(F32)
+        depart_scale = upright[:, 2 * bands + b : 2 * bands + b + 1]
+        depart = depart_scale * (anomaly - upright[:, 3 * bands + b : 3 * bands + b + 1])
+        narrow = depart.astype(BF16)
+        depart = narrow.astype(F32)
         centre = jnp.mean(depart, axis=1, keepdims=True)
         spread = depart - centre
         centre_sum = centre_sum + centre * centre
         spread_sum = spread_sum + spread * spread
         packed = jnp.concatenate([depart[:half], depart[half:]], axis=1)
-        pay_ref[lon, b * half : (b + 1) * half, :] = packed.astype(BF16)
-        tags = jnp.where(lane == 2 * b, col[:half], tags)
-        tags = jnp.where(lane == 2 * b + 1, col[half:], tags)
-    pay_ref[lon, bands * half :, :] = tags.astype(BF16)
+        own_ref[b * half : (b + 1) * half, :] = packed.astype(BF16)
+        row = local_int[b : b + 1]
+        used = mask[b : b + 1] > 0.0
+        same = (col == local[b : b + 1]) & (depart_scale > 0.0) & earlier
+        rank = jnp.sum(jnp.where(same, 1.0, 0.0), axis=0, keepdims=True).astype(jnp.int32)
+        bases = (row, row - (columns - reach), row + first - (cols_ref[b] - reach))
+        marks = []
+        for base in bases:
+            fits = used & (base >= 0) & (base < reach)
+            slot = jnp.where(fits, base * OC + rank, -1)
+            marks.append(jnp.where(slot_ids == slot, 1.0, 0.0))
+        compact = dot(jnp.concatenate(marks, axis=0).astype(BF16), narrow)
+        for kind in range(3):
+            low = kind * ends
+            packed = jnp.concatenate(
+                [compact[low : low + ends // 2], compact[low + ends // 2 : low + ends]], axis=1
+            )
+            ends_buf[kind, b * ends // 2 : (b + 1) * ends // 2, :] = packed.astype(BF16)
     numerator = jnp.sum(centre_sum, axis=0, keepdims=True)
     spread_row = jnp.sum(spread_sum, axis=0, keepdims=True)
     mask_row = jnp.sum(mask, axis=0, keepdims=True)
@@ -129,75 +165,146 @@
         mask_row, axis=1, keepdims=True
     )
     stat_lane = iota((8, LANES), 1)
-    stat_buf[me] = jnp.where(stat_lane == 0, numerator, denominator)
-
-    pl.semaphore_wait(barrier, total - 1)
-
-    def stat_copy(slot, step, other):
+    lat_buf[lat] = jnp.where(stat_lane == 0, numerator, denominator)
+
+    pl.semaphore_wait(barrier, lons + lats - 2)
+
+    def lat_copy(slot, step, other):
         return pltpu.make_async_remote_copy(
-            src_ref=stat_buf.at[slot],
-            dst_ref=stat_buf.at[slot],
-            send_sem=stat_send.at[step],
-            recv_sem=stat_recv.at[slot],
-            device_id=(other // lons, lax.rem(other, lons)),
+            src_ref=lat_buf.at[slot],
+            dst_ref=lat_buf.at[slot],
+            send_sem=lat_send.at[step],
+            recv_sem=lat_recv.at[slot],
+            device_id=(other, lon),
             device_id_type=MESH,
         )
 
-    def pay_copy(slot, step, other):
+    def lon_copy(slot, step, other):
         return pltpu.make_async_remote_copy(
-            src_ref=pay_ref.at[slot],
-            dst_ref=pay_ref.at[slot],
-            send_sem=pay_send.at[step],
-            recv_sem=pay_recv.at[slot],
+            src_ref=lon_buf.at[slot],
+            dst_ref=lon_buf.at[slot],
+            send_sem=lon_send.at[step],
+            recv_sem=lon_recv.at[slot],
             device_id=(lat, other),
             device_id_type=MESH,
         )
 
-    def send_stat(step, carry):
-        stat_copy(me, step, lax.rem(me + step, total)).start()
+    def near_copy(kind, slot, other):
+        return pltpu.make_async_remote_copy(
+            src_ref=ends_buf.at[kind],
+            dst_ref=near_buf.at[slot],
+            send_sem=near_send.at[slot],
+            recv_sem=near_recv.at[slot],
+            device_id=(lat, other),
+            device_id_type=MESH,
+        )
+
+    def head_copy(other):
+        return pltpu.make_async_remote_copy(
+            src_ref=ends_buf.at[0],
+            dst_ref=near_buf.at[2],
+            send_sem=head_send.at[other],
+            recv_sem=head_recv,
+            device_id=(lat, other),
+            device_id_type=MESH,
+        )
+
+    def tail_copy(slot):
+        return pltpu.make_async_remote_copy(
+            src_ref=ends_buf.at[2],
+            dst_ref=tail_buf.at[slot],
+            send_sem=tail_send,
+            recv_sem=tail_recv.at[slot],
+            device_id=(lat, 0),
+            device_id_type=MESH,
+        )
+
+    for step in range(1, lats):
+        lat_copy(lat, step, lax.rem(lat + step, lats)).start()
+
+    @pl.when(lon > 0)
+    def _():
+        tail_copy(lon).start()
+        near_copy(0, 1, lon - 1).start()
+
+    @pl.when(lon == 0)
+    def _():
+        def send(other, carry):
+            head_copy(other).start()
+            return carry
+
+        lax.fori_loop(1, lons, send, 0)
+
+    @pl.when(lon < lons - 1)
+    def _():
+        near_copy(1, 0, lon + 1).start()
+
+    for step in range(1, lats):
+        source = lax.rem(lat + lats - step, lats)
+        lat_copy(source, step, source).wait_recv()
+    lon_buf[lon] = jnp.sum(lat_buf[...], axis=0)
+
+    def send_lon(step, carry):
+        lon_copy(lon, step, lax.rem(lon + step, lons)).start()
         return carry
 
-    def send_pay(step, carry):
-        pay_copy(lon, step, lax.rem(lon + step, lons)).start()
+    lax.fori_loop(1, lons, send_lon, 0)
+    for step in range(1, lats):
+        lat_copy(lat, step, lax.rem(lat + step, lats)).wait_send()
+
+    @pl.when(lon > 0)
+    def _():
+        near_copy(1, 0, lon - 1).wait_recv()
+        head_copy(lon).wait_recv()
+        tail_copy(lon).wait_send()
+        near_copy(0, 1, lon - 1).wait_send()
+
+    @pl.when(lon == 0)
+    def _():
+        def take(other, carry):
+            head_copy(other).wait_send()
+            tail_copy(other).wait_recv()
+            return carry
+
+        lax.fori_loop(1, lons, take, 0)
+
+    @pl.when(lon < lons - 1)
+    def _():
+        near_copy(0, 1, lon + 1).wait_recv()
+        near_copy(1, 0, lon + 1).wait_send()
+
+    side_ref[0] = (
+        near_buf[0].astype(F32) + jnp.sum(tail_buf[...].astype(F32), axis=0)
+    ).astype(BF16)
+    side_ref[1] = near_buf[1]
+    side_ref[2] = near_buf[2]
+
+    def take_lon(step, carry):
+        lon_copy(lon, step, lax.rem(lon + step, lons)).wait_send()
+        source = lax.rem(lon + lons - step, lons)
+        lon_copy(source, step, source).wait_recv()
         return carry
 
-    lax.fori_loop(1, lons, send_pay, 0)
-    lax.fori_loop(1, total, send_stat, 0)
-
-    def take_stat(step, carry):
-        stat_copy(me, step, lax.rem(me + step, total)).wait_send()
-        source = lax.rem(me + total - step, total)
-        stat_copy(source, step, source).wait_recv()
-        return carry
-
-    def take_pay(step, carry):
-        pay_copy(lon, step, lax.rem(lon + step, lons)).wait_send()
-        source = lax.rem(lon + lons - step, lons)
-        pay_copy(source, step, source).wait_recv()
-        return carry
-
-    lax.fori_loop(1, total, take_stat, 0)
-    lax.fori_loop(1, lons, take_pay, 0)
-    stats = jnp.sum(stat_buf[...], axis=0)
+    lax.fori_loop(1, lons, take_lon, 0)
+    stats = jnp.sum(lon_buf[...], axis=0)
     inflation = (stats[:, 0:1] + 1e-06) / stats[:, 1:2]
     shift_ref[...] = jnp.broadcast_to((K - 1) / inflation, (8, LANES))
 
 
-def analysis_kernel(x_ref, pay_ref, shift_ref, cols_ref, out_ref, tags_s, xs, ys, w_s, st_s, rhs_s, gs):
+def analysis_kernel(
+    x_ref, own_ref, side_ref, shift_ref, col_ref, cols_ref, out_ref, xs, ys, w_s, st_s, rhs_s, gs
+):
     lon = lax.axis_index("lon")
     bands, columns, width = x_ref.shape
-    lons, pay_rows, _ = pay_ref.shape
-    half = pay_rows // (bands + 1)
-    held = lons * half
+    half = own_ref.shape[0] // bands
+    quarter = side_ref.shape[1] // bands
+    held = LANES
     obs = 2 * held
+    sides = half + 3 * quarter
     pairs = width // LANES
     groups = columns // GROUP
     span = GROUP * K
     tapering = taper_weights(RADIUS)
-    tags = jnp.concatenate(
-        [pay_ref[j, bands * half :, :] for j in range(lons)], axis=0
-    ).astype(F32)
-    tags_s[...] = jnp.transpose(tags)
     shift = shift_ref[0:1, 0:1]
     low = iota((K, LANES), 1) < K
     low_f = jnp.where(low, 1.0, 0.0)
@@ -225,8 +332,12 @@
         for p in range(pairs):
             xs[:, p, :] = x_ref[b, :, p * LANES : (p + 1) * LANES].astype(F32)
         start = pl.multiple_of(b * half, half)
+        side = pl.multiple_of(b * quarter, quarter)
         block = jnp.concatenate(
-            [pay_ref[j, pl.ds(start, half), :] for j in range(lons)], axis=0
+            [own_ref[pl.ds(start, half), :]]
+            + [side_ref[kind, pl.ds(side, quarter), :] for kind in range(3)]
+            + [jnp.zeros((held - sides, LANES), BF16)],
+            axis=0,
         ).astype(F32)
         turned = jnp.transpose(block)
         depart_t = jnp.concatenate([turned[:K], turned[K:]], axis=1)
@@ -238,14 +349,32 @@
             [jnp.where(low_h, block, rolled), jnp.where(low_h, rolled, block)], axis=0
         )
         rhs_s[...] = (rhs - jnp.mean(rhs, axis=1, keepdims=True)).astype(BF16)
-        col = jnp.concatenate(
-            [tags_s[pl.ds(2 * b, 1), :], tags_s[pl.ds(2 * b + 1, 1), :]], axis=1
-        )
-        owner = (iota((1, obs), 1) % held) // half
-        source = col.astype(jnp.int32) + owner * columns
-        away = source - (lon * columns + iota((columns, obs), 0))
-        away = jnp.where(2 * away > count, away - count, away)
-        away = jnp.where(2 * away < -count, away + count, away)
+        col = col_ref[pl.ds(b, 1), :] - lon * columns
+        col = jnp.concatenate([col, jnp.zeros((1, held - 2 * half), jnp.int32)], axis=1)
+        col = jnp.concatenate([col, jnp.roll(col, -half, axis=1)], axis=1)
+        place = iota((1, obs), 1)
+        spot = place % held
+        slot = spot - half + (place // held) * quarter
+        where_left = slot // OC - (RADIUS - 1)
+        where_right = (slot - quarter) // OC + columns
+        where_head = (slot - 2 * quarter) // OC + count - lon * columns
+        source = jnp.where(
+            spot < half,
+            col,
+            jnp.where(
+                spot < half + quarter,
+                where_left,
+                jnp.where(
+                    spot < half + 2 * quarter,
+                    where_right,
+                    jnp.where(spot < sides, where_head, FAR),
+                ),
+            ),
+        )
+        limit = jnp.where(spot < half, count, FAR)
+        away = source - iota((columns, obs), 0)
+        away = jnp.where(2 * away > limit, away - count, away)
+        away = jnp.where(2 * away < -limit, away + count, away)
         away = jnp.abs(away)
         weight = jnp.zeros((columns, obs), F32)
         for t in range(RADIUS):
@@ -348,46 +477,55 @@
 def per_device(lats, lons, background, band_cols, obs_col, obs_lev, obs_mask, innov, obs_var):
     bands, columns, width = background.shape
     obs = obs_col.shape[1]
-    half = obs // 2
-    pay_rows = (bands + 1) * half
-    total = lats * lons
+    pairs = width // LANES
     vmem = pl.BlockSpec(memory_space=pltpu.VMEM)
-    pay, shift = pl.pallas_call(
+    smem = pl.BlockSpec(memory_space=pltpu.SMEM)
+    dma = pltpu.SemaphoreType.DMA
+    end_rows = bands * END_SLOTS // 2
+    own, side, shift = pl.pallas_call(
         functools.partial(exchange_kernel, lats, lons),
         out_shape=(
-            jax.ShapeDtypeStruct((lons, pay_rows, LANES), BF16),
+            jax.ShapeDtypeStruct((bands * obs // 2, LANES), BF16),
+            jax.ShapeDtypeStruct((3, end_rows, LANES), BF16),
             jax.ShapeDtypeStruct((8, LANES), F32),
         ),
-        in_specs=[vmem] * 6,
-        out_specs=(vmem, vmem),
+        in_specs=[vmem] * 6 + [smem],
+        out_specs=(vmem, vmem, vmem),
         scratch_shapes=[
-            pltpu.VMEM((total, 8, LANES), F32),
-            pltpu.SemaphoreType.DMA((lons,)),
-            pltpu.SemaphoreType.DMA((lons,)),
-            pltpu.SemaphoreType.DMA((total,)),
-            pltpu.SemaphoreType.DMA((total,)),
+            pltpu.VMEM((3, end_rows, LANES), BF16),
+            pltpu.VMEM((3, end_rows, LANES), BF16),
+            pltpu.VMEM((lons, end_rows, LANES), BF16),
+            pltpu.VMEM((lats, 8, LANES), F32),
+            pltpu.VMEM((lons, 8, LANES), F32),
+            dma((2,)),
+            dma((2,)),
+            dma((lons,)),
+            dma,
+            dma,
+            dma((lons,)),
+            dma((lats,)),
+            dma((lats,)),
+            dma((lons,)),
+            dma((lons,)),
         ],
         compiler_params=pltpu.CompilerParams(collective_id=0, has_side_effects=True),
         name="exchange",
-    )(background, obs_col, obs_lev, obs_mask, innov, obs_var)
-    held = lons * half
-    pairs = width // LANES
+    )(background, obs_col, obs_lev, obs_mask, innov, obs_var, band_cols)
     return pl.pallas_call(
         analysis_kernel,
         out_shape=jax.ShapeDtypeStruct(background.shape, BF16),
-        in_specs=[vmem, vmem, vmem, pl.BlockSpec(memory_space=pltpu.SMEM)],
+        in_specs=[vmem] * 5 + [smem],
         out_specs=vmem,
         scratch_shapes=[
-            pltpu.VMEM((LANES, held), F32),
             pltpu.VMEM((columns, pairs, LANES), F32),
             pltpu.VMEM((columns, pairs, LANES), F32),
-            pltpu.VMEM((columns, 2 * held), F32),
-            pltpu.VMEM((K, 2 * held), F32),
-            pltpu.VMEM((2 * held, LANES), BF16),
+            pltpu.VMEM((columns, 2 * LANES), F32),
+            pltpu.VMEM((K, 2 * LANES), F32),
+            pltpu.VMEM((2 * LANES, LANES), BF16),
             pltpu.VMEM((columns // GROUP, K, GROUP * K), F32),
         ],
         name="analysis",
-    )(background, pay, shift, band_cols)
+    )(background, own, side, shift, obs_col, band_cols)
 
 
 def solution(mesh):

time: 49.8 us -> 42.1 us (0.85)
  Pallas kernels: 49.6 us -> 42 us
    pallas_call x1, Pallas kernels: 21.8 us -> 15.7 us  [per_device(): pl.pallas_call(functools.partial(exchange_kernel, lats, lons), out_shape=...]
    pallas_call x1, Pallas kernels: 27.8 us -> 26.3 us  [per_device(): pl.pallas_call(analysis_kernel, out_shape=jax.ShapeDtypeStruct(background...]
where the time goes in v1:
time: 42.1 us; the launch traced here: 42 us
  Pallas kernels  42 us (100%)
    pallas_call x1, Pallas kernels, per_device(): pl.pallas_call(analysis_kernel, out_shape=jax.ShapeDtypeStruct(background...  26.3 us
    pallas_call x1, Pallas kernels, per_device(): pl.pallas_call(functools.partial(exchange_kernel, lats, lons), out_shape=...  15.7 us

profile of v1, /device:TPU:0, one launch (start us, length us, event | category | flops | bytes accessed | tf_op | source)
XLA Modules:
  0.0 42.0 jit_solution(13274821237336804187)
XLA Ops:
  0.0 15.7 %exchange.1 = (bf16[128,128]{1,0:T(8,128)(2,1)}, bf16[3,64,128]{2,1,0:T(8,128)(2,1)}, f32[8,128]{1,0:T(8,128)}) custom-call(bf16[4,32,2560]{2,1,0:T(8,128)(2,1)} %x_ref.3, s32[4,64]{1,0:T(4,128)} %col_ref.3, s32[4,64]{1,0:T(4,128)} %lev_ref.1, s32[4,64]{1,0:T(4,128)} %mask_ref.1, f32[4,64]{1,0:T(4,128)} %innov_ref.1, f32[4,64]{1,0:T(4,128)} %var_ref.1, ...), custom_call_target="tpu_custom_call" | custom-call | tf_op jit(solution)/shard_map/exchange/pallas_call | solution.py:485
  15.7 26.3 %analysis.1 = bf16[4,32,2560]{2,1,0:T(8,128)(2,1)} custom-call(bf16[4,32,2560]{2,1,0:T(8,128)(2,1)} %x_ref.3, bf16[128,128]{1,0:T(8,128)(2,1)} %get-tuple-element.8.own_ref, bf16[3,64,128]{2,1,0:T(8,128)(2,1)} %get-tuple-element.9.side_ref, f32[8,128]{1,0:T(8,128)} %get-tuple-element.10.shift_ref, s32[4,64]{1,0:T(4,128)} %col_ref.3, s32[4]{0:T(128)} %cols_ref.3), custom_call_target="tpu_custom_call" | custom-call | tf_op jit(solution)/shard_map/analysis/pallas_call | solution.py:514

commit v2 on v1

--- a/solution.py
+++ b/solution.py
@@ -311,6 +311,8 @@
     low_b = low_f.astype(BF16)
     high_b = (1.0 - low_f).astype(BF16)
     zero_b = jnp.zeros((K, LANES), BF16)
+    rows_x = xs.shape[0] // columns
+    low_x = iota((rows_x, LANES), 1) < K
     eye = jnp.where(iota((K, span), 0) == iota((K, span), 1) % K, 1.0, 0.0)
 
     def block_diag(mat):
@@ -330,7 +332,8 @@
     def one_band(b, carry):
         count = cols_ref[b]
         for p in range(pairs):
-            xs[:, p, :] = x_ref[b, :, p * LANES : (p + 1) * LANES].astype(F32)
+            strip = x_ref[b, :, p * LANES : (p + 1) * LANES].astype(F32)
+            xs[pl.ds(p, columns, stride=rows_x), :] = strip
         start = pl.multiple_of(b * half, half)
         side = pl.multiple_of(b * quarter, quarter)
         block = jnp.concatenate(
@@ -401,7 +404,7 @@
         inv_frob = 1.0 / frob
         scaling = jnp.sqrt((K - 1.0) * inv_frob)
         beta_all = 1.0 - shift * inv_frob
-        batch = min(4, groups)
+        batch = min(8, groups)
         for first in range(0, groups, batch):
             ids = range(first, first + batch)
             beta = [beta_all[g : g + 1] for g in ids]
@@ -436,38 +439,58 @@
                         for be, s, d, c in zip(beta, square, dev, cube)
                     ]
                     beta = [be * be * (0.75 + 0.25 * be) for be in beta]
-            for i, g in enumerate(ids):
+            full = [ze * eye + r for ze, r in zip(zeta, root)]
+            mean_row = []
+            for g in ids:
                 c0 = g * GROUP
-                row = jnp.concatenate(
-                    [
-                        jnp.where(low[:1], mean_rows[c0 : c0 + 1], mean_rows[c0 + 1 : c0 + 2]),
-                        jnp.where(low[:1], mean_rows[c0 + 2 : c0 + 3], mean_rows[c0 + 3 : c0 + 4]),
-                    ],
-                    axis=1,
+                m = [mean_rows[c : c + 1] for c in range(c0, c0 + GROUP)]
+                mean_row.append(
+                    jnp.concatenate(
+                        [jnp.where(low[:1], m[0], m[1]), jnp.where(low[:1], m[2], m[3])], axis=1
+                    )
                 )
-                full = zeta[i] * eye + root[i]
-                rows = jnp.broadcast_to(row, (8, span)).astype(BF16)
-                half_step = zeta[i] * row + dot(rows, block_diag(root[i].astype(BF16)))[:1]
-                shifted = dot((full * half_step).astype(BF16), ones_bd)
+            half_step = [
+                ze * m
+                + dot(
+                    jnp.broadcast_to(m, (8, span)).astype(BF16), block_diag(r.astype(BF16))
+                )[:1]
+                for ze, m, r in zip(zeta, mean_row, root)
+            ]
+            shifted = [
+                dot((f * h).astype(BF16), ones_bd) for f, h in zip(full, half_step)
+            ]
+            mix = []
+            for f, ze, sh, g in zip(full, zeta, shifted, ids):
                 scale = scaling[g : g + 1]
-                mix = (
-                    scale * full
-                    + (1.0 - scale * zeta[i]) * (1.0 / K)
-                    + shifted * inv_frob[g : g + 1]
+                mix.append(
+                    (
+                        scale * f
+                        + (1.0 - scale * ze) * (1.0 / K)
+                        + sh * inv_frob[g : g + 1]
+                    ).astype(BF16)
                 )
-                for pair in range(GROUP // 2):
-                    two = mix[:, pair * LANES : (pair + 1) * LANES]
-                    swapped = pltpu.roll(two, K, 1).astype(BF16)
-                    two = two.astype(BF16)
-                    for side in range(2):
-                        c = c0 + 2 * pair + side
-                        upper, lower = (two, swapped) if side == 0 else (swapped, two)
-                        apply = jnp.concatenate([upper * low_b, lower * high_b], axis=0)
-                        ys[c] = dot(xs[c].astype(BF16), apply)
+            applied = []
+            for g, mx in zip(ids, mix):
+                c0 = g * GROUP
+                sides_in = []
+                for c in (c0, c0 + 2):
+                    here = xs[c * rows_x : (c + 1) * rows_x, :]
+                    there = xs[(c + 1) * rows_x : (c + 2) * rows_x, :]
+                    even = jnp.where(low_x, here, pltpu.roll(there, K, 1))
+                    odd = jnp.where(low_x, pltpu.roll(here, K, 1), there)
+                    sides_in.append(jnp.concatenate([even, odd], axis=0).astype(BF16))
+                applied.append(dot(jnp.concatenate(sides_in, axis=1), block_diag(mx)))
+            for g, result in zip(ids, applied):
+                c0 = g * GROUP
+                for side, c in enumerate((c0, c0 + 2)):
+                    got = result[:, side * LANES : (side + 1) * LANES]
+                    even, odd = got[:rows_x], got[rows_x:]
+                    ys[c * rows_x : (c + 1) * rows_x, :] = jnp.where(low_x, even, pltpu.roll(odd, K, 1))
+                    ys[(c + 1) * rows_x : (c + 2) * rows_x, :] = jnp.where(low_x, pltpu.roll(even, K, 1), odd)
         keep = lon * columns + iota((columns, LANES), 0) < count
         for p in range(pairs):
             out_ref[b, :, p * LANES : (p + 1) * LANES] = jnp.where(
-                keep, ys[:, p, :], 0.0
+                keep, ys[pl.ds(p, columns, stride=rows_x), :], 0.0
             ).astype(BF16)
         return carry
 
@@ -482,6 +505,7 @@
     smem = pl.BlockSpec(memory_space=pltpu.SMEM)
     dma = pltpu.SemaphoreType.DMA
     end_rows = bands * END_SLOTS // 2
+    padded_pairs = -(-pairs // 8) * 8
     own, side, shift = pl.pallas_call(
         functools.partial(exchange_kernel, lats, lons),
         out_shape=(
@@ -517,8 +541,8 @@
         in_specs=[vmem] * 5 + [smem],
         out_specs=vmem,
         scratch_shapes=[
-            pltpu.VMEM((columns, pairs, LANES), F32),
-            pltpu.VMEM((columns, pairs, LANES), F32),
+            pltpu.VMEM((columns * padded_pairs, LANES), F32),
+            pltpu.VMEM((columns * padded_pairs, LANES), F32),
             pltpu.VMEM((columns, 2 * LANES), F32),
             pltpu.VMEM((K, 2 * LANES), F32),
             pltpu.VMEM((2 * LANES, LANES), BF16),

time: 42.1 us -> 30.1 us (0.71)
  Pallas kernels: 42 us -> 30 us
    pallas_call x1, Pallas kernels: 26.3 us -> 14.2 us  [per_device(): pl.pallas_call(analysis_kernel, out_shape=jax.ShapeDtypeStruct(background...]
where the time goes in v2:
time: 30.1 us; the launch traced here: 30 us
  Pallas kernels  30 us (100%)
    pallas_call x1, Pallas kernels, per_device(): pl.pallas_call(functools.partial(exchange_kernel, lats, lons), out_shape=...  15.7 us
    pallas_call x1, Pallas kernels, per_device(): pl.pallas_call(analysis_kernel, out_shape=jax.ShapeDtypeStruct(background...  14.2 us

profile of v2, /device:TPU:0, one launch (start us, length us, event | category | flops | bytes accessed | tf_op | source)
XLA Modules:
  0.0 30.0 jit_solution(15585721212749436399)
XLA Ops:
  0.0 15.7 %exchange.1 = (bf16[128,128]{1,0:T(8,128)(2,1)}, bf16[3,64,128]{2,1,0:T(8,128)(2,1)}, f32[8,128]{1,0:T(8,128)}) custom-call(bf16[4,32,2560]{2,1,0:T(8,128)(2,1)} %x_ref.3, s32[4,64]{1,0:T(4,128)} %col_ref.3, s32[4,64]{1,0:T(4,128)} %lev_ref.1, s32[4,64]{1,0:T(4,128)} %mask_ref.1, f32[4,64]{1,0:T(4,128)} %innov_ref.1, f32[4,64]{1,0:T(4,128)} %var_ref.1, ...), custom_call_target="tpu_custom_call" | custom-call | tf_op jit(solution)/shard_map/exchange/pallas_call | solution.py:509
  15.7 14.2 %analysis.1 = bf16[4,32,2560]{2,1,0:T(8,128)(2,1)} custom-call(bf16[4,32,2560]{2,1,0:T(8,128)(2,1)} %x_ref.3, bf16[128,128]{1,0:T(8,128)(2,1)} %get-tuple-element.8.own_ref, bf16[3,64,128]{2,1,0:T(8,128)(2,1)} %get-tuple-element.9.side_ref, f32[8,128]{1,0:T(8,128)} %get-tuple-element.10.shift_ref, s32[4,64]{1,0:T(4,128)} %col_ref.3, s32[4]{0:T(128)} %cols_ref.3), custom_call_target="tpu_custom_call" | custom-call | tf_op jit(solution)/shard_map/analysis/pallas_call | solution.py:538
